TPU v7x, 32 devices: a whole 2x2x4 slice. The times are simulated.
32 devices in a mesh: batch: 16 (over z, y, core), rep: 2 (over x).
Axes of the slice: x: 2, y: 2, z: 4, core: 2. Of those that a mesh axis runs over, the one named last changes fastest.
Arguments:
- queries: bfloat16 [2048, 512], P('batch', 'rep'), may hold values from -8 to 8
- passages: bfloat16 [2048, 512], P('batch', 'rep'), may hold values from -8 to 8
- positives: int32 [2048], replicated, may hold values from 0 to 2047, each once
Outputs:
- grad_queries: float32 [2048, 512], P('batch', 'rep')
- grad_passages: float32 [2048, 512], P('batch', 'rep')
Inputs may be any that keep to these rules, and one draw needn't show every extreme that they name: `positives`: each passage is the positive of exactly one query.
All inputs are finite; a program needn't handle non-finite values.
Results may differ from a plain program's by a relative error of at most 0.0013.
Values may be sent and summed in bfloat16 or wider, within the bound.
A program may use at most 128 MiB of HBM per device.

v0:
```python
import functools
import math

import jax
import jax.numpy as jnp
from jax import lax
from jax.experimental import pallas as pl
from jax.experimental.pallas import tpu as pltpu
from jax.sharding import PartitionSpec as P

MESH = pl.DeviceIdType.MESH
F32 = jnp.float32
BF16 = jnp.bfloat16
I16 = jnp.int16


def dot(a, b, da, db):
    return lax.dot_general(a, b, (((da,), (db,)), ((), ())), preferred_element_type=F32)


def as_column(row, lanes):
    return jnp.broadcast_to(row, (lanes, row.shape[1])).T


def kernel(
    Z,
    scale,
    q_ref,
    p_ref,
    pos_hbm,
    gq_ref,
    gp_ref,
    Q,
    Qs,
    PB,
    S,
    W,
    Ws,
    rst,
    rrc,
    cst,
    crc,
    PM,
    pos_ref,
    gqp,
    gqt,
    gqr,
    gqk,
    gqkr,
    gpt,
    gpr,
    gpk,
    gpkr,
    fin,
    q_s,
    q_r,
    p_s,
    p_r,
    f_s,
    f_r,
    h_s,
    h_r,
    r_s,
    r_r,
    c_s,
    c_r,
    w_s,
    w_r,
    gq_s,
    gq_r,
    gp_s,
    gp_r,
    gqk_s,
    gqk_r,
    gpk_s,
    gpk_r,
    in_s,
):
    n, w = q_ref.shape
    b = lax.axis_index("batch")
    x = lax.axis_index("rep")
    z, y, c = b // 4, (b // 2) % 2, b % 2
    rows, cols = 2 * n, Z * n
    blocks = min(Z, 4)
    wide = blocks * n
    chunks = Z // blocks

    def dev(zz, yy, cc, xx):
        return (zz * 4 + yy * 2 + cc, xx)

    def plane(j):
        xx = 1 - x if j & 1 else x
        yy = 1 - y if j & 2 else y
        return xx, yy

    def remote(src, dst, s, r, device):
        return pltpu.make_async_remote_copy(
            src_ref=src, dst_ref=dst, send_sem=s, recv_sem=r, device_id=device, device_id_type=MESH
        )

    def up(dz):
        return (z + dz) % Z

    def down(dz):
        return (z + Z - dz) % Z

    own = c == x
    sibling = dev(z, y, 1 - c, x)

    barrier = pltpu.get_barrier_semaphore()

    q_own = Q.at[x, pl.ds(pl.multiple_of(y * n, n), n)]
    p_in = pltpu.make_async_copy(p_ref, PM, in_s.at[0])
    q_in = pltpu.make_async_copy(q_ref, q_own, in_s.at[1])
    pos_in = pltpu.make_async_copy(pos_hbm, pos_ref, in_s.at[2])
    p_in.start()
    q_in.start()
    pos_in.start()

    def greet(device):
        pl.semaphore_signal(barrier, inc=1, device_id=device, device_id_type=MESH)

    for j in (1, 2, 3):
        xx, yy = plane(j)
        greet(dev(z, yy, c, xx))
    for dz in range(Z):
        if dz:
            greet(dev(up(dz), y, c, x))
            greet(dev(up(dz), y, x, c))
        else:

            @pl.when(jnp.logical_not(own))
            def _():
                greet(dev(z, y, x, c))

        greet(dev(up(dz), y, 1 - c, x))
    p_in.wait()
    q_in.wait()
    pos_in.wait()

    @pl.when(own)
    def _():
        PB[c, pl.ds(pl.multiple_of(z * n, n), n), :] = PM[...]

    pl.semaphore_wait(barrier, 3 + 3 * Z - 1 - own.astype(jnp.int32))

    slot = PB.at[c, pl.ds(pl.multiple_of(z * n, n), n)]

    def p_copy(dz):
        if dz:
            return remote(slot, slot, p_s.at[dz], p_r.at[dz], dev(up(dz), y, c, x))
        return remote(
            PM,
            PB.at[x, pl.ds(pl.multiple_of(z * n, n), n)],
            p_s.at[0],
            p_r.at[0],
            dev(z, y, x, c),
        )

    def q_copy(j):
        xx, yy = plane(j)
        return remote(
            q_own,
            q_own,
            q_s.at[j - 1],
            q_r.at[j - 1],
            dev(z, yy, c, xx),
        )

    p_copies = [p_copy(dz) for dz in range(Z)]
    q_copies = [q_copy(j) for j in (1, 2, 3)]
    def forward(dz):
        zs = down(dz)
        part = PB.at[c, pl.ds(pl.multiple_of(zs * n, n), n)]
        return remote(part, part, f_s.at[dz], f_r.at[dz], sibling)

    forwards = [forward(dz) for dz in range(Z)]

    @pl.when(jnp.logical_not(own))
    def _():
        p_copies[0].start()

    for copy in q_copies:
        copy.start()

    @pl.when(jnp.logical_not(own))
    def _():
        p_copies[0].wait_recv()

    order = list(range(1, Z))
    for dz in order:
        p_copies[dz].start()
    forwards[0].start()

    def span(k, size):
        return pl.ds(k * size if isinstance(k, int) else pl.multiple_of(k * size, size), size)

    def score(dz):
        forwards[dz].wait_recv()
        zs = down(dz)
        at = span(zs, n)
        s = (dot(Q[0], PB[0, at, :], 1, 1) + dot(Q[1], PB[1, at, :], 1, 1)) * scale
        S[:, at] = s
        top = jnp.max(s, axis=0, keepdims=True)
        cst[:, at] = top
        cst[:, span(zs + Z, n)] = jnp.sum(jnp.exp(s - top), axis=0, keepdims=True)

    for copy in q_copies:
        copy.wait_recv()
    half = remote(Q.at[1 - c], Qs, h_s, h_r, sibling)
    half.start()
    for dz in order:
        p_copies[dz].wait_recv()
        forwards[dz].start()
        score(dz - 1)
    score(Z - 1)

    col_copies = []
    for dz in range(Z):
        for dc in (0, 1):
            if dz or dc:
                k = dz * 2 + dc
                col_copies.append(
                    remote(
                        cst,
                        crc.at[k],
                        c_s.at[k],
                        c_r.at[k],
                        dev(up(dz), y, 1 - c if dc else c, x),
                    )
                )
                col_copies[-1].start()

    def row_high(k, high):
        return jnp.maximum(high, jnp.max(S[:, span(k, wide)], axis=1, keepdims=True))

    def row_total(k, total):
        s = S[:, span(k, wide)]
        return total + jnp.sum(jnp.exp(s - highest), axis=1, keepdims=True)

    low, zero = jnp.full((rows, 1), -1e30, F32), jnp.zeros((rows, 1), F32)
    if chunks == 1:
        highest = row_high(0, low)
        running = (highest, row_total(0, zero))
    else:
        highest = lax.fori_loop(0, chunks, row_high, low)
        running = (highest, lax.fori_loop(0, chunks, row_total, zero))

    def as_row(column):
        return jnp.broadcast_to(column, (rows, 128)).T[0:1, :]

    rst[:, 0:rows] = as_row(running[0])
    rst[:, rows : 2 * rows] = as_row(running[1])
    row_copies = []
    for j in (1, 2, 3):
        xx, yy = plane(j)
        row_copies.append(
            remote(rst, rrc.at[j], r_s.at[j - 1], r_r.at[j - 1], dev(z, yy, c, xx))
        )
        row_copies[-1].start()

    places = jnp.concatenate(
        [
            as_column(pos_ref[pl.ds(z * 4 + yy * 2 + c, 1), :].astype(F32), 128)
            for yy in (0, 1)
        ],
        axis=0,
    )

    for copy in row_copies:
        copy.wait_recv()
    high = rst[:, 0:rows]
    for j in (1, 2, 3):
        high = jnp.maximum(high, rrc[j, :, 0:rows])
    total = rst[:, rows : 2 * rows] * jnp.exp(rst[:, 0:rows] - high)
    for j in (1, 2, 3):
        total += rrc[j, :, rows : 2 * rows] * jnp.exp(rrc[j, :, 0:rows] - high)
    row_norm = as_column(high + jnp.log(total), 128)

    for copy in col_copies:
        copy.wait_recv()
    high = cst[:, 0:cols]
    for k in range(1, 2 * Z):
        high = jnp.maximum(high, crc[k, :, 0:cols])
    total = cst[:, cols : 2 * cols] * jnp.exp(cst[:, 0:cols] - high)
    for k in range(1, 2 * Z):
        total += crc[k, :, cols : 2 * cols] * jnp.exp(crc[k, :, 0:cols] - high)
    crc[0, :, 0:cols] = high + jnp.log(total)

    lane = lax.broadcasted_iota(jnp.int32, (rows, n), 1).astype(F32)

    shares = []
    turn = order + [0]
    for dz in turn:
        zb = up(dz)
        at = span(zb, n)
        s = S[:, at]
        col_norm = crc[0, :, at]
        base = lax.convert_element_type((zb * 4 + y * 2 + x) * n, F32)
        hit = jnp.where(places - lane == base, 2.0, 0.0)
        W[dz] = (jnp.exp(s - row_norm) + jnp.exp(s - col_norm) - hit).astype(BF16)
        shares.append(remote(W.at[dz], Ws.at[dz], w_s.at[dz], w_r.at[dz], sibling))
        shares[-1].start()

    def pack(value, to, step, k):
        top = jnp.maximum(jnp.max(jnp.abs(value), axis=0, keepdims=True), 1e-30)
        to[k] = jnp.round(value * (32766.0 / top)).astype(jnp.int32).astype(I16)
        step[k] = top * (1.0 / 32766.0)

    def unpack(at, step, k):
        return at[k].astype(jnp.int32).astype(F32) * step[k]

    def gp_copy(dz):
        device = dev(up(dz), y, x, c)
        return (
            remote(gpt.at[dz], gpr.at[dz], gp_s.at[dz], gp_r.at[dz], device),
            remote(gpk.at[dz], gpkr.at[dz], gpk_s.at[dz], gpk_r.at[dz], device),
        )

    gp_copies = [gp_copy(dz) for dz in range(Z)]

    def gp_send(value, dz):
        pack(value, gpt, gpk, dz)
        for copy in gp_copies[dz]:
            copy.start()

    def query_terms(h):
        def term(k):
            return dot(W[k], PB[h, span(up(k), n), :], 1, 0)

        if Z <= 4:
            return sum(term(k) for k in range(1, Z)) + term(0)
        return lax.fori_loop(0, Z, lambda k, t: t + term(k), jnp.zeros((rows, w), F32))

    for h in (0, 1):
        gqp[h] = query_terms(h)
    gq_copies = []
    for j in (3, 1, 2):
        xx, yy = plane(j)
        pack(gqp[xx, pl.ds(pl.multiple_of(yy * n, n), n), :], gqt, gqk, j - 1)
        for src, dst, ss, rr in ((gqt, gqr, gq_s, gq_r), (gqk, gqkr, gqk_s, gqk_r)):
            gq_copies.append(
                remote(
                    src.at[j - 1],
                    dst.at[j - 1],
                    ss.at[j - 1],
                    rr.at[j - 1],
                    dev(z, yy, c, xx),
                )
            )
            gq_copies[-1].start()

    half.wait_recv()
    for dz, share in zip(turn, shares):
        share.wait_recv()
        value = dot(W[dz], Q[c], 0, 0) + dot(Ws[dz], Qs[...], 0, 0)
        if dz:
            gp_send(value, dz)
        else:
            fin[...] = value

            @pl.when(jnp.logical_not(own))
            def _():
                gp_send(fin[...], 0)

    for copy in gq_copies:
        copy.wait_recv()
    total = gqp[x, pl.ds(pl.multiple_of(y * n, n), n), :]
    for j in range(3):
        total += unpack(gqr, gqkr, j)
    gq_ref[...] = total

    @pl.when(jnp.logical_not(own))
    def _():
        for copy in gp_copies[0]:
            copy.wait_recv()
        fin[...] = unpack(gpr, gpkr, 0)

    for dz in order:
        for copy in gp_copies[dz]:
            copy.wait_recv()
    total = fin[...]
    for dz in range(1, Z):
        total += unpack(gpr, gpkr, dz)
    gp_ref[...] = total

    @pl.when(jnp.logical_not(own))
    def _():
        p_copies[0].wait_send()
        for copy in gp_copies[0]:
            copy.wait_send()

    for dz in order:
        p_copies[dz].wait_send()
        for copy in gp_copies[dz]:
            copy.wait_send()
    for copy in q_copies + forwards + [half] + shares + col_copies + row_copies + gq_copies:
        copy.wait_send()


def local(queries, passages, positives):
    n, w = queries.shape
    batch_count = lax.axis_size("batch")
    Z = batch_count // 4
    scale = 1.0 / math.sqrt(w * lax.axis_size("rep"))
    rows, cols = 2 * n, Z * n
    vmem = pl.BlockSpec(memory_space=pltpu.VMEM)
    dma = pltpu.SemaphoreType.DMA
    hbm = pl.BlockSpec(memory_space=pltpu.HBM)
    operands = (queries, passages, positives.reshape(batch_count, n))
    grad_queries, grad_passages = pl.pallas_call(
        functools.partial(kernel, Z, scale),
        out_shape=(
            jax.ShapeDtypeStruct((n, w), F32),
            jax.ShapeDtypeStruct((n, w), F32),
        ),
        in_specs=[hbm] * 3,
        out_specs=(vmem, vmem),
        scratch_shapes=[
            pltpu.VMEM((2, rows, w), BF16),
            pltpu.VMEM((rows, w), BF16),
            pltpu.VMEM((2, cols, w), BF16),
            pltpu.VMEM((rows, cols), F32),
            pltpu.VMEM((Z, rows, n), BF16),
            pltpu.VMEM((Z, rows, n), BF16),
            pltpu.VMEM((1, 2 * rows), F32),
            pltpu.VMEM((4, 1, 2 * rows), F32),
            pltpu.VMEM((1, 2 * cols), F32),
            pltpu.VMEM((2 * Z, 1, 2 * cols), F32),
            pltpu.VMEM((n, w), BF16),
            pltpu.VMEM((batch_count, n), jnp.int32),
            pltpu.VMEM((2, rows, w), F32),
            pltpu.VMEM((3, n, w), I16),
            pltpu.VMEM((3, n, w), I16),
            pltpu.VMEM((3, 1, w), F32),
            pltpu.VMEM((3, 1, w), F32),
            pltpu.VMEM((Z, n, w), I16),
            pltpu.VMEM((Z, n, w), I16),
            pltpu.VMEM((Z, 1, w), F32),
            pltpu.VMEM((Z, 1, w), F32),
            pltpu.VMEM((n, w), F32),
            dma((3,)),
            dma((3,)),
            dma((Z,)),
            dma((Z,)),
            dma((Z,)),
            dma((Z,)),
            dma,
            dma,
            dma((3,)),
            dma((3,)),
            dma((2 * Z,)),
            dma((2 * Z,)),
            dma((Z,)),
            dma((Z,)),
            dma((3,)),
            dma((3,)),
            dma((Z,)),
            dma((Z,)),
            dma((3,)),
            dma((3,)),
            dma((Z,)),
            dma((Z,)),
            dma((3,)),
        ],
        compiler_params=pltpu.CompilerParams(collective_id=0, has_side_effects=True, vmem_limit_bytes=6 * 2**20 + 40 * rows * cols),
    )(*(pltpu.with_memory_space_constraint(a, pltpu.HBM) for a in operands))
    return grad_queries * scale, grad_passages * scale


def solution(mesh):
    in_specs = (P("batch", "rep"), P("batch", "rep"), P())
    out_specs = (P("batch", "rep"), P("batch", "rep"))
    return jax.shard_map(local, mesh=mesh, in_specs=in_specs, out_specs=out_specs, check_vma=False)
```

profile of v0, /device:TPU:0, one launch (start us, length us, event | category | flops | bytes accessed | tf_op | source)
XLA Modules:
  0.0 30.1 jit_solution(13705910049877134265)
XLA Ops:
  0.6 28.7 %shard_map.50 = (f32[128,256]{1,0:T(8,128)S(1)}, f32[128,256]{1,0:T(8,128)S(1)}) custom-call(bf16[128,256]{1,0:T(8,128)(2,1)} %q_ref.1, bf16[128,256]{1,0:T(8,128)(2,1)} %p_ref.1, s32[16,128]{1,0:T(8,128)} %bitcast.1), custom_call_target="tpu_custom_call" | custom-call | tf_op jit(solution)/shard_map/pallas_call | solution.py:411
  29.4 0.7 %broadcast_multiply_fusion = (f32[128,256]{1,0:T(8,128)}, f32[128,256]{1,0:T(8,128)}) fusion(f32[128,256]{1,0:T(8,128)S(1)} %get-tuple-element.5, f32[128,256]{1,0:T(8,128)S(1)} %get-tuple-element.4), kind=kLoop, calls=%fused_computation | loop fusion | flops 65536 | bytes 524288 | tf_op jit(solution)/shard_map/mul | solution.py:468
where the time goes:
time: 30.2 us; the launch traced here: 30.1 us
  Pallas kernels  28.7 us (95%)
  other arithmetic  0.72 us (2%)
  between operations  0.64 us (2%)
    pallas_call x1, Pallas kernels, local(): pl.pallas_call(functools.partial(kernel, Z, scale), out_shape=(jax.ShapeD...  28.7 us
    mul x1, other arithmetic, local(): return (grad_queries * scale, grad_passages * scale)  0.72 us

commit v1 on v0

v1 whole, which is shorter than its diff:
```python
import functools
import math

import jax
import jax.numpy as jnp
from jax import lax
from jax.experimental import pallas as pl
from jax.experimental.pallas import tpu as pltpu
from jax.sharding import PartitionSpec as P

MESH = pl.DeviceIdType.MESH
F32 = jnp.float32
BF16 = jnp.bfloat16
I16 = jnp.int16


def dot(a, b, da, db):
    return lax.dot_general(a, b, (((da,), (db,)), ((), ())), preferred_element_type=F32)


def as_column(row, lanes):
    return jnp.broadcast_to(row, (lanes, row.shape[1])).T


def kernel(
    Z,
    scale,
    q_ref,
    p_ref,
    pos_hbm,
    gq_ref,
    gp_ref,
    Q,
    Qs,
    PB,
    S,
    W,
    Ws,
    rst,
    rrc,
    cst,
    crc,
    PM,
    pos_ref,
    gqp,
    gqt,
    gqr,
    gqk,
    gqkr,
    gpt,
    gpr,
    gpk,
    gpkr,
    near,
    line,
    rest,
    in_s,
    q_s,
    q_r,
    p_s,
    p_r,
    f_s,
    f_r,
    h_s,
    h_r,
    r_s,
    r_r,
    c_s,
    c_r,
    w_s,
    w_r,
    gq_s,
    gq_r,
    gp_s,
    gp_r,
    gqk_s,
    gqk_r,
    gpk_s,
    gpk_r,
):
    n, w = q_ref.shape
    b = lax.axis_index("batch")
    x = lax.axis_index("rep")
    z, y, c = b // 4, (b // 2) % 2, b % 2
    rows, cols = 2 * n, Z * n
    blocks = min(Z, 4)
    wide = blocks * n
    chunks = Z // blocks

    def dev(zz, yy, cc, xx):
        return (zz * 4 + yy * 2 + cc, xx)

    def plane(j):
        xx = 1 - x if j & 1 else x
        yy = 1 - y if j & 2 else y
        return xx, yy

    def remote(src, dst, s, r, device):
        return pltpu.make_async_remote_copy(
            src_ref=src, dst_ref=dst, send_sem=s, recv_sem=r, device_id=device, device_id_type=MESH
        )

    def span(k, size):
        return pl.ds(k * size if isinstance(k, int) else pl.multiple_of(k * size, size), size)

    def up(dz):
        return (z + dz) % Z

    own = c == x
    crossed = jnp.logical_not(own)
    sibling = dev(z, y, 1 - c, x)

    def target(zz):
        return dev(zz, y, x, c)

    barrier = pltpu.get_barrier_semaphore()

    q_own = Q.at[x, span(y, n)]
    p_in = pltpu.make_async_copy(p_ref, PM, in_s.at[0])
    q_in = pltpu.make_async_copy(q_ref, q_own, in_s.at[1])
    pos_in = pltpu.make_async_copy(pos_hbm, pos_ref, in_s.at[2])
    q_in.start()
    p_in.start()
    pos_in.start()

    def greet(sem, device):
        pl.semaphore_signal(sem, inc=1, device_id=device, device_id_type=MESH)

    place = 2 * y + x
    pairs = []
    for j in (1, 2, 3):
        xx, yy = plane(j)
        pairs.append((2 * yy + xx < place, dev(z, yy, c, xx), near.at[j - 1]))
    pairs.append((c == 0, sibling, rest))
    for dz in range(1, Z):
        zz = up(dz)
        pairs.append((zz < z, target(zz), line.at[z]))
        for cc in (0, 1):
            pairs.append((zz < z, dev(zz, y, cc, x), rest))
    first = jnp.logical_and(crossed, c < x)
    last = jnp.logical_and(crossed, c > x)
    for earlier, device, _ in pairs:

        @pl.when(jnp.logical_not(earlier))
        def _():
            greet(barrier, device)

    @pl.when(last)
    def _():
        greet(barrier, target(z))

    greetings = place + 3 * z + (1 - c) + first.astype(jnp.int32)

    @pl.when(greetings > 0)
    def _():
        pl.semaphore_wait(barrier, greetings)

    for earlier, device, sem in pairs:

        @pl.when(earlier)
        def _():
            greet(sem, device)

    @pl.when(first)
    def _():
        greet(line.at[z], target(z))

    p_in.wait()
    p_block = PB.at[x, span(z, n)]

    def p_copy(zz):
        return remote(PM, p_block, p_s, p_r.at[z], target(zz))

    for k in range(Z - 1):

        @pl.when(k < z)
        def _():
            p_copy(k).start()

    q_in.wait()
    pos_in.wait()

    @pl.when(own)
    def _():
        PB[c, span(z, n), :] = PM[...]

    q_copies = []
    for j in (1, 3, 2):
        xx, yy = plane(j)
        q_copies.append(remote(q_own, q_own, q_s, q_r, dev(z, yy, c, xx)))

        @pl.when(2 * yy + xx > place)
        def _():
            pl.semaphore_wait(near.at[j - 1], 1)

        q_copies[-1].start()

    @pl.when(last)
    def _():
        pl.semaphore_wait(line.at[z], 1)

    @pl.when(crossed)
    def _():
        p_copy(z).start()

    for k in range(1, Z):

        @pl.when(k > z)
        def _():
            pl.semaphore_wait(line.at[k], 1)
            p_copy(k).start()

    answers = 2 * (Z - 1 - z) + c

    @pl.when(answers > 0)
    def _():
        pl.semaphore_wait(rest, answers)

    def part(zz):
        return PB.at[c, span(zz, n)]

    def forward(zz):
        return remote(part(zz), part(zz), f_s, f_r.at[zz], sibling)

    def nth(k):
        return lax.select(k < z, z - 1 - k, jnp.int32(k))

    def score(k):
        zz = nth(k)
        forward(zz).wait_recv()
        at = span(zz, n)
        s = (dot(Q[0], PB[0, at, :], 1, 1) + dot(Q[1], PB[1, at, :], 1, 1)) * scale
        S[:, at] = s
        top = jnp.max(s, axis=0, keepdims=True)
        cst[:, at] = top
        cst[:, span(zz + Z, n)] = jnp.sum(jnp.exp(s - top), axis=0, keepdims=True)

    half = remote(Q.at[1 - c], Qs, h_s, h_r, sibling)

    @pl.when(own)
    def _():
        forward(z).start()

    def arrive(k):
        zz = nth(k)

        @pl.when(jnp.logical_or(zz != z, crossed))
        def _():
            pltpu.make_async_copy(PM, part(zz), p_r.at[zz]).wait()
            forward(zz).start()

    arrive(0)
    arrive(1)
    pltpu.make_async_copy(gqr, gqr, q_r).wait()
    half.start()
    for k in range(2, Z):
        if k < Z - 1:
            score(k - 2)
        arrive(k)
    for k in range(Z - 3, Z):
        score(k)

    col_copies = []
    for dz in range(Z):
        for dc in (0, 1):
            if dz or dc:
                k = dz * 2 + dc
                col_copies.append(
                    remote(cst, crc.at[k - 1], c_s, c_r, dev(up(dz), y, 1 - c if dc else c, x))
                )
                col_copies[-1].start()

    def row_high(k, high):
        return jnp.maximum(high, jnp.max(S[:, span(k, wide)], axis=1, keepdims=True))

    def row_total(k, total):
        s = S[:, span(k, wide)]
        return total + jnp.sum(jnp.exp(s - highest), axis=1, keepdims=True)

    low, zero = jnp.full((rows, 1), -1e30, F32), jnp.zeros((rows, 1), F32)
    if chunks == 1:
        highest = row_high(0, low)
        running = (highest, row_total(0, zero))
    else:
        highest = lax.fori_loop(0, chunks, row_high, low)
        running = (highest, lax.fori_loop(0, chunks, row_total, zero))

    def as_row(column):
        return jnp.broadcast_to(column, (rows, 128)).T[0:1, :]

    rst[:, 0:rows] = as_row(running[0])
    rst[:, rows : 2 * rows] = as_row(running[1])
    row_copies = []
    for j in (1, 2, 3):
        xx, yy = plane(j)
        row_copies.append(remote(rst, rrc.at[j - 1], r_s, r_r, dev(z, yy, c, xx)))
        row_copies[-1].start()

    places = jnp.concatenate(
        [
            as_column(pos_ref[pl.ds(z * 4 + yy * 2 + c, 1), :].astype(F32), 128)
            for yy in (0, 1)
        ],
        axis=0,
    )

    pltpu.make_async_copy(rrc, rrc, r_r).wait()
    high = rst[:, 0:rows]
    for j in range(3):
        high = jnp.maximum(high, rrc[j, :, 0:rows])
    total = rst[:, rows : 2 * rows] * jnp.exp(rst[:, 0:rows] - high)
    for j in range(3):
        total += rrc[j, :, rows : 2 * rows] * jnp.exp(rrc[j, :, 0:rows] - high)
    row_norm = as_column(high + jnp.log(total), 128)

    pltpu.make_async_copy(crc, crc, c_r).wait()
    high = cst[:, 0:cols]
    for k in range(2 * Z - 1):
        high = jnp.maximum(high, crc[k, :, 0:cols])
    total = cst[:, cols : 2 * cols] * jnp.exp(cst[:, 0:cols] - high)
    for k in range(2 * Z - 1):
        total += crc[k, :, cols : 2 * cols] * jnp.exp(crc[k, :, 0:cols] - high)
    col_norms = high + jnp.log(total)

    lane = lax.broadcasted_iota(jnp.int32, (rows, n), 1).astype(F32)

    shares = []
    for k in range(Z):
        at = span(k, n)
        s = S[:, at]
        col_norm = col_norms[:, k * n : (k + 1) * n]
        base = lax.convert_element_type((k * 4 + y * 2 + x) * n, F32)
        hit = jnp.where(places - lane == base, 2.0, 0.0)
        W[k] = (jnp.exp(s - row_norm) + jnp.exp(s - col_norm) - hit).astype(BF16)
        shares.append(remote(W.at[k], Ws.at[k], w_s, w_r.at[k], sibling))
        shares[-1].start()

    def pack(value):
        top = jnp.maximum(jnp.max(jnp.abs(value), axis=0, keepdims=True), 1e-30)
        return jnp.round(value * (32766.0 / top)).astype(jnp.int32).astype(I16), top * (1.0 / 32766.0)

    def unpack(at, step, k):
        return at[k].astype(jnp.int32).astype(F32) * step[k]

    def query_terms(h):
        def term(k):
            return dot(W[k], PB[h, span(k, n), :], 1, 0)

        if Z <= 4:
            return sum(term(k) for k in range(1, Z)) + term(0)
        return lax.fori_loop(0, Z, lambda k, t: t + term(k), jnp.zeros((rows, w), F32))

    for h in (0, 1):
        gqp[h] = query_terms(h)

    for yy, xx in ((0, 0), (0, 1), (1, 0), (1, 1)):

        @pl.when(jnp.logical_or(yy != y, xx != x))
        def _():
            j = (x + xx) % 2 + 2 * ((y + yy) % 2) - 1
            gqt[j], gqk[j] = pack(gqp[xx, yy * n : (yy + 1) * n, :])
            device = dev(z, yy, c, xx)
            remote(gqt.at[j], gqr.at[j], gq_s, gq_r, device).start()
            remote(gqk.at[j], gqkr.at[j], gqk_s, gqk_r, device).start()

    half.wait_recv()
    for k in range(Z):
        shares[k].wait_recv()
        packed, step = pack(dot(W[k], Q[c], 0, 0) + dot(Ws[k], Qs[...], 0, 0))
        away = jnp.logical_or(z != k, crossed)

        @pl.when(away)
        def _():
            gpt[k], gpk[k] = packed, step
            remote(gpt.at[k], gpr.at[z], gp_s, gp_r, target(k)).start()
            remote(gpk.at[k], gpkr.at[z], gpk_s, gpk_r, target(k)).start()

        @pl.when(jnp.logical_not(away))
        def _():
            gpr[k], gpkr[k] = packed, step

    pltpu.make_async_copy(gqr, gqr, gq_r).wait()
    pltpu.make_async_copy(gqkr, gqkr, gqk_r).wait()
    total = gqp[x, span(y, n), :]
    for j in range(3):
        total += unpack(gqr, gqkr, j)
    gq_ref[...] = total

    def gp_wait(count, data, step):
        pltpu.make_async_copy(gpr.at[pl.ds(0, count)], gpr.at[pl.ds(0, count)], data).wait()
        pltpu.make_async_copy(gpkr.at[pl.ds(0, count)], gpkr.at[pl.ds(0, count)], step).wait()

    def per_count(body):
        @pl.when(own)
        def _():
            body(Z - 1)

        @pl.when(crossed)
        def _():
            body(Z)

    per_count(lambda count: gp_wait(count, gp_r, gpk_r))
    gp_ref[...] = sum(unpack(gpr, gpkr, k) for k in range(Z))

    def p_wait(count):
        pltpu.make_async_copy(PB.at[0, pl.ds(0, count * n)], PB.at[0, pl.ds(0, count * n)], p_s).wait()
        gp_wait(count, gp_s, gpk_s)

    per_count(p_wait)
    for ref, sem in (
        (gqr, q_s),
        (PB.at[0], f_s),
        (W, w_s),
        (crc, c_s),
        (rrc, r_s),
        (gqt, gq_s),
        (gqk, gqk_s),
        (Qs, h_s),
    ):
        pltpu.make_async_copy(ref, ref, sem).wait()


def local(queries, passages, positives):
    n, w = queries.shape
    batch_count = lax.axis_size("batch")
    Z = batch_count // 4
    scale = 1.0 / math.sqrt(w * lax.axis_size("rep"))
    rows, cols = 2 * n, Z * n
    vmem = pl.BlockSpec(memory_space=pltpu.VMEM)
    dma = pltpu.SemaphoreType.DMA
    regular = pltpu.SemaphoreType.REGULAR
    hbm = pl.BlockSpec(memory_space=pltpu.HBM)
    operands = (queries, passages, positives.reshape(batch_count, n))
    grad_queries, grad_passages = pl.pallas_call(
        functools.partial(kernel, Z, scale),
        out_shape=(
            jax.ShapeDtypeStruct((n, w), F32),
            jax.ShapeDtypeStruct((n, w), F32),
        ),
        in_specs=[hbm] * 3,
        out_specs=(vmem, vmem),
        scratch_shapes=[
            pltpu.VMEM((2, rows, w), BF16),
            pltpu.VMEM((rows, w), BF16),
            pltpu.VMEM((2, cols, w), BF16),
            pltpu.VMEM((rows, cols), F32),
            pltpu.VMEM((Z, rows, n), BF16),
            pltpu.VMEM((Z, rows, n), BF16),
            pltpu.VMEM((1, 2 * rows), F32),
            pltpu.VMEM((3, 1, 2 * rows), F32),
            pltpu.VMEM((1, 2 * cols), F32),
            pltpu.VMEM((2 * Z - 1, 1, 2 * cols), F32),
            pltpu.VMEM((n, w), BF16),
            pltpu.VMEM((batch_count, n), jnp.int32),
            pltpu.VMEM((2, rows, w), F32),
            pltpu.VMEM((3, n, w), I16),
            pltpu.VMEM((3, n, w), I16),
            pltpu.VMEM((3, 1, w), F32),
            pltpu.VMEM((3, 1, w), F32),
            pltpu.VMEM((Z, n, w), I16),
            pltpu.VMEM((Z, n, w), I16),
            pltpu.VMEM((Z, 1, w), F32),
            pltpu.VMEM((Z, 1, w), F32),
            regular((3,)),
            regular((Z,)),
            regular,
            dma((3,)),
            dma,
            dma,
            dma,
            dma((Z,)),
            dma,
            dma((Z,)),
            dma,
            dma,
            dma,
            dma,
            dma,
            dma,
            dma,
            dma((Z,)),
            dma,
            dma,
            dma,
            dma,
            dma,
            dma,
            dma,
            dma,
        ],
        compiler_params=pltpu.CompilerParams(collective_id=0, has_side_effects=True, vmem_limit_bytes=6 * 2**20 + 40 * rows * cols),
    )(*(pltpu.with_memory_space_constraint(a, pltpu.HBM) for a in operands))
    return grad_queries * scale, grad_passages * scale


def solution(mesh):
    in_specs = (P("batch", "rep"), P("batch", "rep"), P())
    out_specs = (P("batch", "rep"), P("batch", "rep"))
    return jax.shard_map(local, mesh=mesh, in_specs=in_specs, out_specs=out_specs, check_vma=False)
```

time: 30.2 us -> 29 us (0.960)
  Pallas kernels: 28.7 us -> 27.2 us
    pallas_call x1, Pallas kernels: 28.7 us -> 27.2 us  [local(): pl.pallas_call(functools.partial(kernel, Z, scale), out_shape=(jax.ShapeD...]
where the time goes in v1:
time: 29 us; the launch traced here: 28.6 us
  Pallas kernels  27.2 us (94%)
  other arithmetic  0.72 us (2%)
  between operations  0.64 us (2%)
    pallas_call x1, Pallas kernels, local(): pl.pallas_call(functools.partial(kernel, Z, scale), out_shape=(jax.ShapeD...  27.2 us
    mul x1, other arithmetic, local(): return (grad_queries * scale, grad_passages * scale)  0.72 us

profile of v1, /device:TPU:0, one launch (start us, length us, event | category | flops | bytes accessed | tf_op | source)
XLA Modules:
  0.0 28.6 jit_solution(14986684132257522189)
XLA Ops:
  0.6 27.2 %shard_map.50 = (f32[128,256]{1,0:T(8,128)S(1)}, f32[128,256]{1,0:T(8,128)S(1)}) custom-call(bf16[128,256]{1,0:T(8,128)(2,1)} %q_ref.1, bf16[128,256]{1,0:T(8,128)(2,1)} %p_ref.1, s32[16,128]{1,0:T(8,128)} %bitcast.1), custom_call_target="tpu_custom_call" | custom-call | tf_op jit(solution)/shard_map/pallas_call | solution.py:434
  27.9 0.7 %broadcast_multiply_fusion = (f32[128,256]{1,0:T(8,128)}, f32[128,256]{1,0:T(8,128)}) fusion(f32[128,256]{1,0:T(8,128)S(1)} %get-tuple-element.5, f32[128,256]{1,0:T(8,128)S(1)} %get-tuple-element.4), kind=kLoop, calls=%fused_computation | loop fusion | flops 65536 | bytes 524288 | tf_op jit(solution)/shard_map/mul | solution.py:493

commit v2 on v1

--- a/solution.py
+++ b/solution.py
@@ -203,12 +203,19 @@
     def _():
         p_copy(z).start()
 
-    for k in range(1, Z):
-
-        @pl.when(k > z)
-        def _():
-            pl.semaphore_wait(line.at[k], 1)
-            p_copy(k).start()
+    def send_later(zz):
+        pl.semaphore_wait(line.at[zz], 1)
+        p_copy(zz).start()
+
+    for k in range(2, Z):
+
+        @pl.when(k > z + 1)
+        def _():
+            send_later(k)
+
+    @pl.when(z < Z - 1)
+    def _():
+        send_later(z + 1)
 
     answers = 2 * (Z - 1 - z) + c
 
@@ -223,17 +230,19 @@
         return remote(part(zz), part(zz), f_s, f_r.at[zz], sibling)
 
     def nth(k):
-        return lax.select(k < z, z - 1 - k, jnp.int32(k))
-
-    def score(k):
-        zz = nth(k)
-        forward(zz).wait_recv()
-        at = span(zz, n)
-        s = (dot(Q[0], PB[0, at, :], 1, 1) + dot(Q[1], PB[1, at, :], 1, 1)) * scale
-        S[:, at] = s
-        top = jnp.max(s, axis=0, keepdims=True)
-        cst[:, at] = top
-        cst[:, span(zz + Z, n)] = jnp.sum(jnp.exp(s - top), axis=0, keepdims=True)
+        return lax.select(k < Z - z, z + k, jnp.int32(Z - 1 - k))
+
+    def scores(*ks):
+        for k in ks:
+            forward(nth(k)).wait_recv()
+        for k in ks:
+            zz = nth(k)
+            at = span(zz, n)
+            s = (dot(Q[0], PB[0, at, :], 1, 1) + dot(Q[1], PB[1, at, :], 1, 1)) * scale
+            S[:, at] = s
+            top = jnp.max(s, axis=0, keepdims=True)
+            cst[:, at] = top
+            cst[:, span(zz + Z, n)] = jnp.sum(jnp.exp(s - top), axis=0, keepdims=True)
 
     half = remote(Q.at[1 - c], Qs, h_s, h_r, sibling)
 
@@ -253,12 +262,11 @@
     arrive(1)
     pltpu.make_async_copy(gqr, gqr, q_r).wait()
     half.start()
+    scores(0, 1)
     for k in range(2, Z):
-        if k < Z - 1:
-            score(k - 2)
         arrive(k)
-    for k in range(Z - 3, Z):
-        score(k)
+    for k in range(2, Z, 2):
+        scores(k, k + 1)
 
     col_copies = []
     for dz in range(Z):
@@ -353,18 +361,23 @@
     for h in (0, 1):
         gqp[h] = query_terms(h)
 
-    for yy, xx in ((0, 0), (0, 1), (1, 0), (1, 1)):
-
-        @pl.when(jnp.logical_or(yy != y, xx != x))
-        def _():
-            j = (x + xx) % 2 + 2 * ((y + yy) % 2) - 1
-            gqt[j], gqk[j] = pack(gqp[xx, yy * n : (yy + 1) * n, :])
-            device = dev(z, yy, c, xx)
-            remote(gqt.at[j], gqr.at[j], gq_s, gq_r, device).start()
-            remote(gqk.at[j], gqkr.at[j], gqk_s, gqk_r, device).start()
+    def gq_send(yy, xx):
+        j = (x + xx) % 2 + 2 * ((y + yy) % 2) - 1
+        gqt[j], gqk[j] = pack(gqp[xx, yy * n : (yy + 1) * n, :])
+        device = dev(z, yy, c, xx)
+        remote(gqt.at[j], gqr.at[j], gq_s, gq_r, device).start()
+        remote(gqk.at[j], gqkr.at[j], gqk_s, gqk_r, device).start()
+
+    quarters = ((0, 0), (0, 1), (1, 0), (1, 1))
+    for yy, xx in quarters:
+
+        @pl.when(jnp.logical_and(yy != y, xx == x))
+        def _():
+            gq_send(yy, xx)
 
     half.wait_recv()
-    for k in range(Z):
+
+    def gp_send(k):
         shares[k].wait_recv()
         packed, step = pack(dot(W[k], Q[c], 0, 0) + dot(Ws[k], Qs[...], 0, 0))
         away = jnp.logical_or(z != k, crossed)
@@ -378,6 +391,16 @@
         @pl.when(jnp.logical_not(away))
         def _():
             gpr[k], gpkr[k] = packed, step
+
+    gp_send(0)
+    for yy, xx in quarters:
+
+        @pl.when(xx != x)
+        def _():
+            gq_send(yy, xx)
+
+    for k in range(1, Z):
+        gp_send(k)
 
     pltpu.make_async_copy(gqr, gqr, gq_r).wait()
     pltpu.make_async_copy(gqkr, gqkr, gqk_r).wait()

time: 29 us -> 29.9 us (1.031)
  Pallas kernels: 27.2 us -> 28.3 us
    pallas_call x1, Pallas kernels: 27.2 us -> 28.3 us  [local(): pl.pallas_call(functools.partial(kernel, Z, scale), out_shape=(jax.ShapeD...]
where the time goes in v2:
time: 29.9 us; the launch traced here: 29.7 us
  Pallas kernels  28.3 us (95%)
  other arithmetic  0.72 us (2%)
  between operations  0.64 us (2%)
    pallas_call x1, Pallas kernels, local(): pl.pallas_call(functools.partial(kernel, Z, scale), out_shape=(jax.ShapeD...  28.3 us
    mul x1, other arithmetic, local(): return (grad_queries * scale, grad_passages * scale)  0.72 us

profile of v2, /device:TPU:0, one launch (start us, length us, event | category | flops | bytes accessed | tf_op | source)
XLA Modules:
  0.0 29.7 jit_solution(16874745580129160035)
XLA Ops:
  0.6 28.3 %shard_map.50 = (f32[128,256]{1,0:T(8,128)S(1)}, f32[128,256]{1,0:T(8,128)S(1)}) custom-call(bf16[128,256]{1,0:T(8,128)(2,1)} %q_ref.1, bf16[128,256]{1,0:T(8,128)(2,1)} %p_ref.1, s32[16,128]{1,0:T(8,128)} %bitcast.1), custom_call_target="tpu_custom_call" | custom-call | tf_op jit(solution)/shard_map/pallas_call | solution.py:457
  29.0 0.7 %broadcast_multiply_fusion = (f32[128,256]{1,0:T(8,128)}, f32[128,256]{1,0:T(8,128)}) fusion(f32[128,256]{1,0:T(8,128)S(1)} %get-tuple-element.5, f32[128,256]{1,0:T(8,128)S(1)} %get-tuple-element.4), kind=kLoop, calls=%fused_computation | loop fusion | flops 65536 | bytes 524288 | tf_op jit(solution)/shard_map/mul | solution.py:516

commit v3 on v2

--- a/solution.py
+++ b/solution.py
@@ -12,6 +12,7 @@
 F32 = jnp.float32
 BF16 = jnp.bfloat16
 I16 = jnp.int16
+TURNS = ((0, 1, 3, 2), (0, 3, 2, 1), (0, 3, 1, 2), (0, 2, 1, 3))
 
 
 def dot(a, b, da, db):
@@ -34,6 +35,7 @@
     Qs,
     PB,
     S,
+    A,
     W,
     Ws,
     rst,
@@ -83,9 +85,6 @@
     x = lax.axis_index("rep")
     z, y, c = b // 4, (b // 2) % 2, b % 2
     rows, cols = 2 * n, Z * n
-    blocks = min(Z, 4)
-    wide = blocks * n
-    chunks = Z // blocks
 
     def dev(zz, yy, cc, xx):
         return (zz * 4 + yy * 2 + cc, xx)
@@ -106,12 +105,12 @@
     def up(dz):
         return (z + dz) % Z
 
-    own = c == x
+    own = c == 1 - x
     crossed = jnp.logical_not(own)
     sibling = dev(z, y, 1 - c, x)
 
     def target(zz):
-        return dev(zz, y, x, c)
+        return dev(zz, y, 1 - x, 1 - c)
 
     barrier = pltpu.get_barrier_semaphore()
 
@@ -137,8 +136,8 @@
         pairs.append((zz < z, target(zz), line.at[z]))
         for cc in (0, 1):
             pairs.append((zz < z, dev(zz, y, cc, x), rest))
-    first = jnp.logical_and(crossed, c < x)
-    last = jnp.logical_and(crossed, c > x)
+    first = jnp.logical_and(crossed, x == 1)
+    last = jnp.logical_and(crossed, x == 0)
     for earlier, device, _ in pairs:
 
         @pl.when(jnp.logical_not(earlier))
@@ -171,6 +170,10 @@
     def p_copy(zz):
         return remote(PM, p_block, p_s, p_r.at[z], target(zz))
 
+    @pl.when(first)
+    def _():
+        p_copy(z).start()
+
     for k in range(Z - 1):
 
         @pl.when(k < z)
@@ -182,7 +185,12 @@
 
     @pl.when(own)
     def _():
-        PB[c, span(z, n), :] = PM[...]
+        PB[x, span(z, n), :] = PM[...]
+
+    @pl.when(last)
+    def _():
+        pl.semaphore_wait(line.at[z], 1)
+        p_copy(z).start()
 
     q_copies = []
     for j in (1, 3, 2):
@@ -195,27 +203,23 @@
 
         q_copies[-1].start()
 
-    @pl.when(last)
-    def _():
-        pl.semaphore_wait(line.at[z], 1)
-
-    @pl.when(crossed)
-    def _():
-        p_copy(z).start()
-
     def send_later(zz):
         pl.semaphore_wait(line.at[zz], 1)
         p_copy(zz).start()
 
+    @pl.when(jnp.logical_and(z > 0, z < Z - 1))
+    def _():
+        send_later(z + 1)
+
     for k in range(2, Z):
 
         @pl.when(k > z + 1)
         def _():
             send_later(k)
 
-    @pl.when(z < Z - 1)
-    def _():
-        send_later(z + 1)
+    @pl.when(z == 0)
+    def _():
+        send_later(1)
 
     answers = 2 * (Z - 1 - z) + c
 
@@ -224,7 +228,7 @@
         pl.semaphore_wait(rest, answers)
 
     def part(zz):
-        return PB.at[c, span(zz, n)]
+        return PB.at[1 - c, span(zz, n)]
 
     def forward(zz):
         return remote(part(zz), part(zz), f_s, f_r.at[zz], sibling)
@@ -235,6 +239,7 @@
     def scores(*ks):
         for k in ks:
             forward(nth(k)).wait_recv()
+        parts = []
         for k in ks:
             zz = nth(k)
             at = span(zz, n)
@@ -243,8 +248,19 @@
             top = jnp.max(s, axis=0, keepdims=True)
             cst[:, at] = top
             cst[:, span(zz + Z, n)] = jnp.sum(jnp.exp(s - top), axis=0, keepdims=True)
-
-    half = remote(Q.at[1 - c], Qs, h_s, h_r, sibling)
+            parts.append(s)
+        return parts
+
+    def row_part(parts, running):
+        high = jnp.max(functools.reduce(jnp.maximum, parts), axis=1, keepdims=True)
+        if running is not None:
+            high = jnp.maximum(high, running[0])
+        total = jnp.sum(sum(jnp.exp(s - high) for s in parts), axis=1, keepdims=True)
+        if running is not None:
+            total += running[1] * jnp.exp(running[0] - high)
+        return high, total
+
+    half = remote(Q.at[c], Qs, h_s, h_r, sibling)
 
     @pl.when(own)
     def _():
@@ -258,15 +274,14 @@
             pltpu.make_async_copy(PM, part(zz), p_r.at[zz]).wait()
             forward(zz).start()
 
-    arrive(0)
-    arrive(1)
+    for k in range(Z):
+        arrive(k)
     pltpu.make_async_copy(gqr, gqr, q_r).wait()
     half.start()
-    scores(0, 1)
-    for k in range(2, Z):
-        arrive(k)
-    for k in range(2, Z, 2):
-        scores(k, k + 1)
+    running = None
+    for k in range(0, Z - 2, 2):
+        running = row_part(scores(k, k + 1), running)
+    parts = scores(Z - 2, Z - 1)
 
     col_copies = []
     for dz in range(Z):
@@ -278,20 +293,7 @@
                 )
                 col_copies[-1].start()
 
-    def row_high(k, high):
-        return jnp.maximum(high, jnp.max(S[:, span(k, wide)], axis=1, keepdims=True))
-
-    def row_total(k, total):
-        s = S[:, span(k, wide)]
-        return total + jnp.sum(jnp.exp(s - highest), axis=1, keepdims=True)
-
-    low, zero = jnp.full((rows, 1), -1e30, F32), jnp.zeros((rows, 1), F32)
-    if chunks == 1:
-        highest = row_high(0, low)
-        running = (highest, row_total(0, zero))
-    else:
-        highest = lax.fori_loop(0, chunks, row_high, low)
-        running = (highest, lax.fori_loop(0, chunks, row_total, zero))
+    running = row_part(parts, running)
 
     def as_row(column):
         return jnp.broadcast_to(column, (rows, 128)).T[0:1, :]
@@ -321,6 +323,12 @@
         total += rrc[j, :, rows : 2 * rows] * jnp.exp(rrc[j, :, 0:rows] - high)
     row_norm = as_column(high + jnp.log(total), 128)
 
+    lane = lax.broadcasted_iota(jnp.int32, (rows, n), 1).astype(F32)
+    for k in range(Z):
+        base = lax.convert_element_type((k * 4 + y * 2 + 1 - x) * n, F32)
+        hit = jnp.where(places - lane == base, 2.0, 0.0)
+        A[k] = jnp.exp(S[:, span(k, n)] - row_norm) - hit
+
     pltpu.make_async_copy(crc, crc, c_r).wait()
     high = cst[:, 0:cols]
     for k in range(2 * Z - 1):
@@ -328,20 +336,23 @@
     total = cst[:, cols : 2 * cols] * jnp.exp(cst[:, 0:cols] - high)
     for k in range(2 * Z - 1):
         total += crc[k, :, cols : 2 * cols] * jnp.exp(crc[k, :, 0:cols] - high)
-    col_norms = high + jnp.log(total)
-
-    lane = lax.broadcasted_iota(jnp.int32, (rows, n), 1).astype(F32)
-
-    shares = []
-    for k in range(Z):
-        at = span(k, n)
-        s = S[:, at]
-        col_norm = col_norms[:, k * n : (k + 1) * n]
-        base = lax.convert_element_type((k * 4 + y * 2 + x) * n, F32)
-        hit = jnp.where(places - lane == base, 2.0, 0.0)
-        W[k] = (jnp.exp(s - row_norm) + jnp.exp(s - col_norm) - hit).astype(BF16)
-        shares.append(remote(W.at[k], Ws.at[k], w_s, w_r.at[k], sibling))
-        shares[-1].start()
+    crc[0, :, 0:cols] = high + jnp.log(total)
+
+    def turn(i):
+        if Z != 4:
+            return jnp.int32(i)
+        first_z, second_z, third_z, fourth_z = (row[i] for row in TURNS)
+        low = lax.select(z == 0, jnp.int32(first_z), jnp.int32(second_z))
+        high = lax.select(z == 2, jnp.int32(third_z), jnp.int32(fourth_z))
+        return lax.select(z < 2, low, high)
+
+    def share(k):
+        return remote(W.at[k], Ws.at[k], w_s, w_r.at[k], sibling)
+
+    for i in range(Z):
+        k = turn(i)
+        W[k] = (A[k] + jnp.exp(S[:, span(k, n)] - crc[0, :, span(k, n)])).astype(BF16)
+        share(k).start()
 
     def pack(value):
         top = jnp.maximum(jnp.max(jnp.abs(value), axis=0, keepdims=True), 1e-30)
@@ -355,11 +366,8 @@
             return dot(W[k], PB[h, span(k, n), :], 1, 0)
 
         if Z <= 4:
-            return sum(term(k) for k in range(1, Z)) + term(0)
+            return dot(jnp.concatenate([W[k] for k in range(Z)], axis=1), PB[h], 1, 0)
         return lax.fori_loop(0, Z, lambda k, t: t + term(k), jnp.zeros((rows, w), F32))
-
-    for h in (0, 1):
-        gqp[h] = query_terms(h)
 
     def gq_send(yy, xx):
         j = (x + xx) % 2 + 2 * ((y + yy) % 2) - 1
@@ -368,18 +376,21 @@
         remote(gqt.at[j], gqr.at[j], gq_s, gq_r, device).start()
         remote(gqk.at[j], gqkr.at[j], gqk_s, gqk_r, device).start()
 
-    quarters = ((0, 0), (0, 1), (1, 0), (1, 1))
-    for yy, xx in quarters:
-
-        @pl.when(jnp.logical_and(yy != y, xx == x))
+    for h in (0, 1):
+        gqp[h] = query_terms(h)
+    for yy, xx in ((0, 0), (0, 1), (1, 0), (1, 1)):
+
+        @pl.when(jnp.logical_or(yy != y, xx != x))
         def _():
             gq_send(yy, xx)
 
     half.wait_recv()
 
-    def gp_send(k):
-        shares[k].wait_recv()
-        packed, step = pack(dot(W[k], Q[c], 0, 0) + dot(Ws[k], Qs[...], 0, 0))
+    for i in range(Z):
+        k = turn(i)
+        mine = dot(W[k], Q[1 - c], 0, 0)
+        share(k).wait_recv()
+        packed, step = pack(mine + dot(Ws[k], Qs[...], 0, 0))
         away = jnp.logical_or(z != k, crossed)
 
         @pl.when(away)
@@ -391,16 +402,6 @@
         @pl.when(jnp.logical_not(away))
         def _():
             gpr[k], gpkr[k] = packed, step
-
-    gp_send(0)
-    for yy, xx in quarters:
-
-        @pl.when(xx != x)
-        def _():
-            gq_send(yy, xx)
-
-    for k in range(1, Z):
-        gp_send(k)
 
     pltpu.make_async_copy(gqr, gqr, gq_r).wait()
     pltpu.make_async_copy(gqkr, gqkr, gqk_r).wait()
@@ -467,6 +468,7 @@
             pltpu.VMEM((rows, w), BF16),
             pltpu.VMEM((2, cols, w), BF16),
             pltpu.VMEM((rows, cols), F32),
+            pltpu.VMEM((Z, rows, n), F32),
             pltpu.VMEM((Z, rows, n), BF16),
             pltpu.VMEM((Z, rows, n), BF16),
             pltpu.VMEM((1, 2 * rows), F32),

time: 29.9 us -> 28.2 us (0.943)
  Pallas kernels: 28.3 us -> 26.6 us
    pallas_call x1, Pallas kernels: 28.3 us -> 26.6 us  [local(): pl.pallas_call(functools.partial(kernel, Z, scale), out_shape=(jax.ShapeD...]
where the time goes in v3:
time: 28.2 us; the launch traced here: 28 us
  Pallas kernels  26.6 us (94%)
  other arithmetic  0.72 us (3%)
  between operations  0.64 us (2%)
    pallas_call x1, Pallas kernels, local(): pl.pallas_call(functools.partial(kernel, Z, scale), out_shape=(jax.ShapeD...  26.6 us
    mul x1, other arithmetic, local(): return (grad_queries * scale, grad_passages * scale)  0.72 us

profile of v3, /device:TPU:0, one launch (start us, length us, event | category | flops | bytes accessed | tf_op | source)
XLA Modules:
  0.0 28.0 jit_solution(13937809507023925813)
XLA Ops:
  0.6 26.6 %shard_map.50 = (f32[128,256]{1,0:T(8,128)S(1)}, f32[128,256]{1,0:T(8,128)S(1)}) custom-call(bf16[128,256]{1,0:T(8,128)(2,1)} %q_ref.1, bf16[128,256]{1,0:T(8,128)(2,1)} %p_ref.1, s32[16,128]{1,0:T(8,128)} %bitcast.1), custom_call_target="tpu_custom_call" | custom-call | tf_op jit(solution)/shard_map/pallas_call | solution.py:458
  27.3 0.7 %broadcast_multiply_fusion = (f32[128,256]{1,0:T(8,128)}, f32[128,256]{1,0:T(8,128)}) fusion(f32[128,256]{1,0:T(8,128)S(1)} %get-tuple-element.5, f32[128,256]{1,0:T(8,128)S(1)} %get-tuple-element.4), kind=kLoop, calls=%fused_computation | loop fusion | flops 65536 | bytes 524288 | tf_op jit(solution)/shard_map/mul | solution.py:518

commit v4 on v3

--- a/solution.py
+++ b/solution.py
@@ -79,6 +79,8 @@
     gqk_r,
     gpk_s,
     gpk_r,
+    d_r,
+    dk_r,
 ):
     n, w = q_ref.shape
     b = lax.axis_index("batch")
@@ -127,7 +129,7 @@
 
     place = 2 * y + x
     pairs = []
-    for j in (1, 2, 3):
+    for j in (1, 2):
         xx, yy = plane(j)
         pairs.append((2 * yy + xx < place, dev(z, yy, c, xx), near.at[j - 1]))
     pairs.append((c == 0, sibling, rest))
@@ -148,7 +150,7 @@
     def _():
         greet(barrier, target(z))
 
-    greetings = place + 3 * z + (1 - c) + first.astype(jnp.int32)
+    greetings = x + y + 3 * z + (1 - c) + first.astype(jnp.int32)
 
     @pl.when(greetings > 0)
     def _():
@@ -193,9 +195,9 @@
         p_copy(z).start()
 
     q_copies = []
-    for j in (1, 3, 2):
+    for j in (1, 2):
         xx, yy = plane(j)
-        q_copies.append(remote(q_own, q_own, q_s, q_r, dev(z, yy, c, xx)))
+        q_copies.append(remote(q_own, q_own, q_s, q_r.at[j - 1], dev(z, yy, c, xx)))
 
         @pl.when(2 * yy + xx > place)
         def _():
@@ -226,6 +228,10 @@
     @pl.when(answers > 0)
     def _():
         pl.semaphore_wait(rest, answers)
+
+    q_copies[0].wait_recv()
+    q_far = Q.at[1 - x, span(y, n)]
+    remote(q_far, q_far, q_s, q_r.at[1], dev(z, 1 - y, c, x)).start()
 
     def part(zz):
         return PB.at[1 - c, span(zz, n)]
@@ -276,7 +282,7 @@
 
     for k in range(Z):
         arrive(k)
-    pltpu.make_async_copy(gqr, gqr, q_r).wait()
+    pltpu.make_async_copy(Q.at[0], Q.at[0], q_r.at[1]).wait()
     half.start()
     running = None
     for k in range(0, Z - 2, 2):
@@ -369,20 +375,26 @@
             return dot(jnp.concatenate([W[k] for k in range(Z)], axis=1), PB[h], 1, 0)
         return lax.fori_loop(0, Z, lambda k, t: t + term(k), jnp.zeros((rows, w), F32))
 
-    def gq_send(yy, xx):
-        j = (x + xx) % 2 + 2 * ((y + yy) % 2) - 1
-        gqt[j], gqk[j] = pack(gqp[xx, yy * n : (yy + 1) * n, :])
-        device = dev(z, yy, c, xx)
-        remote(gqt.at[j], gqr.at[j], gq_s, gq_r, device).start()
-        remote(gqk.at[j], gqkr.at[j], gqk_s, gqk_r, device).start()
+    def gq_send(j, value, slot, data, step, device):
+        gqt[j], gqk[j] = pack(value)
+        remote(gqt.at[j], gqr.at[slot], gq_s, data, device).start()
+        remote(gqk.at[j], gqkr.at[slot], gqk_s, step, device).start()
 
     for h in (0, 1):
         gqp[h] = query_terms(h)
-    for yy, xx in ((0, 0), (0, 1), (1, 0), (1, 1)):
-
-        @pl.when(jnp.logical_or(yy != y, xx != x))
-        def _():
-            gq_send(yy, xx)
+    beside, across = dev(z, 1 - y, c, x), dev(z, y, c, 1 - x)
+    corner = dev(z, 1 - y, c, lax.select(c == 1, x, 1 - x))
+
+    def gq_across(more):
+        gq_send(2, gqp[1 - x, span(y, n), :] + more, 2, gq_r.at[1], gqk_r.at[1], across)
+
+    gq_send(0, gqp[1 - x, span(1 - y, n), :], 0, d_r, dk_r, corner)
+
+    @pl.when(c == 0)
+    def _():
+        gq_across(0.0)
+
+    gq_send(1, gqp[x, span(1 - y, n), :], 1, gq_r.at[0], gqk_r.at[0], beside)
 
     half.wait_recv()
 
@@ -403,12 +415,18 @@
         def _():
             gpr[k], gpkr[k] = packed, step
 
-    pltpu.make_async_copy(gqr, gqr, gq_r).wait()
-    pltpu.make_async_copy(gqkr, gqkr, gqk_r).wait()
-    total = gqp[x, span(y, n), :]
-    for j in range(3):
-        total += unpack(gqr, gqkr, j)
-    gq_ref[...] = total
+    pltpu.make_async_copy(PM, PM, d_r).wait()
+    pltpu.make_async_copy(gqk.at[0], gqk.at[0], dk_r).wait()
+
+    @pl.when(c == 1)
+    def _():
+        gq_across(unpack(gqr, gqkr, 0))
+
+    for j in (0, 1):
+        pltpu.make_async_copy(PM, PM, gq_r.at[j]).wait()
+        pltpu.make_async_copy(gqk.at[0], gqk.at[0], gqk_r.at[j]).wait()
+    total = gqp[x, span(y, n), :] + unpack(gqr, gqkr, 1) + unpack(gqr, gqkr, 2)
+    gq_ref[...] = total + unpack(gqr, gqkr, 0) * (1 - c).astype(F32)
 
     def gp_wait(count, data, step):
         pltpu.make_async_copy(gpr.at[pl.ds(0, count)], gpr.at[pl.ds(0, count)], data).wait()
@@ -486,12 +504,12 @@
             pltpu.VMEM((Z, n, w), I16),
             pltpu.VMEM((Z, 1, w), F32),
             pltpu.VMEM((Z, 1, w), F32),
-            regular((3,)),
+            regular((2,)),
             regular((Z,)),
             regular,
             dma((3,)),
             dma,
-            dma,
+            dma((2,)),
             dma,
             dma((Z,)),
             dma,
@@ -505,9 +523,11 @@
             dma,
             dma((Z,)),
             dma,
-            dma,
-            dma,
-            dma,
+            dma((2,)),
+            dma,
+            dma,
+            dma,
+            dma((2,)),
             dma,
             dma,
             dma,

time: 28.2 us -> 27.7 us (0.982)
  Pallas kernels: 26.6 us -> 26.2 us
    pallas_call x1, Pallas kernels: 26.6 us -> 26.2 us  [local(): pl.pallas_call(functools.partial(kernel, Z, scale), out_shape=(jax.ShapeD...]
where the time goes in v4:
time: 27.7 us; the launch traced here: 27.5 us
  Pallas kernels  26.2 us (95%)
  other arithmetic  0.72 us (3%)
  between operations  0.64 us (2%)
    pallas_call x1, Pallas kernels, local(): pl.pallas_call(functools.partial(kernel, Z, scale), out_shape=(jax.ShapeD...  26.2 us
    mul x1, other arithmetic, local(): return (grad_queries * scale, grad_passages * scale)  0.72 us

profile of v4, /device:TPU:0, one launch (start us, length us, event | category | flops | bytes accessed | tf_op | source)
XLA Modules:
  0.0 27.5 jit_solution(13394044963234378470)
XLA Ops:
  0.6 26.2 %shard_map.50 = (f32[128,256]{1,0:T(8,128)S(1)}, f32[128,256]{1,0:T(8,128)S(1)}) custom-call(bf16[128,256]{1,0:T(8,128)(2,1)} %q_ref.1, bf16[128,256]{1,0:T(8,128)(2,1)} %p_ref.1, s32[16,128]{1,0:T(8,128)} %bitcast.1), custom_call_target="tpu_custom_call" | custom-call | tf_op jit(solution)/shard_map/pallas_call | solution.py:476
  26.8 0.7 %broadcast_multiply_fusion = (f32[128,256]{1,0:T(8,128)}, f32[128,256]{1,0:T(8,128)}) fusion(f32[128,256]{1,0:T(8,128)S(1)} %get-tuple-element.5, f32[128,256]{1,0:T(8,128)S(1)} %get-tuple-element.4), kind=kLoop, calls=%fused_computation | loop fusion | flops 65536 | bytes 524288 | tf_op jit(solution)/shard_map/mul | solution.py:538

commit v5 on v4

--- a/solution.py
+++ b/solution.py
@@ -17,6 +17,15 @@
 
 def dot(a, b, da, db):
     return lax.dot_general(a, b, (((da,), (db,)), ((), ())), preferred_element_type=F32)
+
+
+def sent_bytes(n, w, Z, crossed=True):
+    block, step = 2 * n * w, 4 * w
+    blocks = 3 + (Z - 1 + crossed) + Z + 2 + 3 + (Z - 1 + crossed)
+    steps = 3 + (Z - 1 + crossed)
+    weights = Z * 2 * n * n * 2
+    stats = (2 * Z - 1) * 2 * Z * n * 4 + 3 * 4 * n * 4
+    return blocks * block + steps * step + weights + stats
 
 
 def as_column(row, lanes):
@@ -44,6 +53,7 @@
     crc,
     PM,
     pos_ref,
+    span_ref,
     gqp,
     gqt,
     gqr,
@@ -57,30 +67,17 @@
     line,
     rest,
     in_s,
-    q_s,
+    out_s,
     q_r,
-    p_s,
     p_r,
-    f_s,
     f_r,
-    h_s,
     h_r,
-    r_s,
     r_r,
-    c_s,
     c_r,
-    w_s,
     w_r,
-    gq_s,
     gq_r,
-    gp_s,
     gp_r,
-    gqk_s,
-    gqk_r,
-    gpk_s,
-    gpk_r,
     d_r,
-    dk_r,
 ):
     n, w = q_ref.shape
     b = lax.axis_index("batch")
@@ -103,6 +100,12 @@
 
     def span(k, size):
         return pl.ds(k * size if isinstance(k, int) else pl.multiple_of(k * size, size), size)
+
+    def settle(sem, size):
+        ref = span_ref.at[:, pl.ds(0, size // 4)]
+        pltpu.make_async_copy(ref, ref, sem).wait()
+
+    packed_bytes = 2 * n * w + 4 * w
 
     def up(dz):
         return (z + dz) % Z
@@ -170,7 +173,7 @@
     p_block = PB.at[x, span(z, n)]
 
     def p_copy(zz):
-        return remote(PM, p_block, p_s, p_r.at[z], target(zz))
+        return remote(PM, p_block, out_s, p_r.at[z], target(zz))
 
     @pl.when(first)
     def _():
@@ -197,7 +200,7 @@
     q_copies = []
     for j in (1, 2):
         xx, yy = plane(j)
-        q_copies.append(remote(q_own, q_own, q_s, q_r.at[j - 1], dev(z, yy, c, xx)))
+        q_copies.append(remote(q_own, q_own, out_s, q_r.at[j - 1], dev(z, yy, c, xx)))
 
         @pl.when(2 * yy + xx > place)
         def _():
@@ -231,20 +234,20 @@
 
     q_copies[0].wait_recv()
     q_far = Q.at[1 - x, span(y, n)]
-    remote(q_far, q_far, q_s, q_r.at[1], dev(z, 1 - y, c, x)).start()
+    remote(q_far, q_far, out_s, q_r.at[1], dev(z, 1 - y, c, x)).start()
 
     def part(zz):
         return PB.at[1 - c, span(zz, n)]
 
-    def forward(zz):
-        return remote(part(zz), part(zz), f_s, f_r.at[zz], sibling)
+    def forward(k):
+        zz = nth(k)
+        return remote(part(zz), part(zz), out_s, f_r.at[k // 2], sibling)
 
     def nth(k):
         return lax.select(k < Z - z, z + k, jnp.int32(Z - 1 - k))
 
     def scores(*ks):
-        for k in ks:
-            forward(nth(k)).wait_recv()
+        pltpu.make_async_copy(Q.at[0], Q.at[0], f_r.at[ks[0] // 2]).wait()
         parts = []
         for k in ks:
             zz = nth(k)
@@ -266,11 +269,11 @@
             total += running[1] * jnp.exp(running[0] - high)
         return high, total
 
-    half = remote(Q.at[c], Qs, h_s, h_r, sibling)
+    half = remote(Q.at[c], Qs, out_s, h_r, sibling)
 
     @pl.when(own)
     def _():
-        forward(z).start()
+        forward(0).start()
 
     def arrive(k):
         zz = nth(k)
@@ -278,7 +281,7 @@
         @pl.when(jnp.logical_or(zz != z, crossed))
         def _():
             pltpu.make_async_copy(PM, part(zz), p_r.at[zz]).wait()
-            forward(zz).start()
+            forward(k).start()
 
     for k in range(Z):
         arrive(k)
@@ -295,7 +298,7 @@
             if dz or dc:
                 k = dz * 2 + dc
                 col_copies.append(
-                    remote(cst, crc.at[k - 1], c_s, c_r, dev(up(dz), y, 1 - c if dc else c, x))
+                    remote(cst, crc.at[k - 1], out_s, c_r, dev(up(dz), y, 1 - c if dc else c, x))
                 )
                 col_copies[-1].start()
 
@@ -309,7 +312,7 @@
     row_copies = []
     for j in (1, 2, 3):
         xx, yy = plane(j)
-        row_copies.append(remote(rst, rrc.at[j - 1], r_s, r_r, dev(z, yy, c, xx)))
+        row_copies.append(remote(rst, rrc.at[j - 1], out_s, r_r, dev(z, yy, c, xx)))
         row_copies[-1].start()
 
     places = jnp.concatenate(
@@ -353,7 +356,7 @@
         return lax.select(z < 2, low, high)
 
     def share(k):
-        return remote(W.at[k], Ws.at[k], w_s, w_r.at[k], sibling)
+        return remote(W.at[k], Ws.at[k], out_s, w_r.at[k], sibling)
 
     for i in range(Z):
         k = turn(i)
@@ -377,8 +380,8 @@
 
     def gq_send(j, value, slot, data, step, device):
         gqt[j], gqk[j] = pack(value)
-        remote(gqt.at[j], gqr.at[slot], gq_s, data, device).start()
-        remote(gqk.at[j], gqkr.at[slot], gqk_s, step, device).start()
+        remote(gqt.at[j], gqr.at[slot], out_s, data, device).start()
+        remote(gqk.at[j], gqkr.at[slot], out_s, step, device).start()
 
     for h in (0, 1):
         gqp[h] = query_terms(h)
@@ -386,15 +389,15 @@
     corner = dev(z, 1 - y, c, lax.select(c == 1, x, 1 - x))
 
     def gq_across(more):
-        gq_send(2, gqp[1 - x, span(y, n), :] + more, 2, gq_r.at[1], gqk_r.at[1], across)
-
-    gq_send(0, gqp[1 - x, span(1 - y, n), :], 0, d_r, dk_r, corner)
+        gq_send(2, gqp[1 - x, span(y, n), :] + more, 2, gq_r.at[1], gq_r.at[1], across)
+
+    gq_send(0, gqp[1 - x, span(1 - y, n), :], 0, d_r, d_r, corner)
 
     @pl.when(c == 0)
     def _():
         gq_across(0.0)
 
-    gq_send(1, gqp[x, span(1 - y, n), :], 1, gq_r.at[0], gqk_r.at[0], beside)
+    gq_send(1, gqp[x, span(1 - y, n), :], 1, gq_r.at[0], gq_r.at[0], beside)
 
     half.wait_recv()
 
@@ -408,30 +411,24 @@
         @pl.when(away)
         def _():
             gpt[k], gpk[k] = packed, step
-            remote(gpt.at[k], gpr.at[z], gp_s, gp_r, target(k)).start()
-            remote(gpk.at[k], gpkr.at[z], gpk_s, gpk_r, target(k)).start()
+            remote(gpt.at[k], gpr.at[z], out_s, gp_r, target(k)).start()
+            remote(gpk.at[k], gpkr.at[z], out_s, gp_r, target(k)).start()
 
         @pl.when(jnp.logical_not(away))
         def _():
             gpr[k], gpkr[k] = packed, step
 
-    pltpu.make_async_copy(PM, PM, d_r).wait()
-    pltpu.make_async_copy(gqk.at[0], gqk.at[0], dk_r).wait()
+    settle(d_r, packed_bytes)
 
     @pl.when(c == 1)
     def _():
         gq_across(unpack(gqr, gqkr, 0))
 
     for j in (0, 1):
-        pltpu.make_async_copy(PM, PM, gq_r.at[j]).wait()
-        pltpu.make_async_copy(gqk.at[0], gqk.at[0], gqk_r.at[j]).wait()
+        settle(gq_r.at[j], packed_bytes)
     total = gqp[x, span(y, n), :] + unpack(gqr, gqkr, 1) + unpack(gqr, gqkr, 2)
     gq_ref[...] = total + unpack(gqr, gqkr, 0) * (1 - c).astype(F32)
 
-    def gp_wait(count, data, step):
-        pltpu.make_async_copy(gpr.at[pl.ds(0, count)], gpr.at[pl.ds(0, count)], data).wait()
-        pltpu.make_async_copy(gpkr.at[pl.ds(0, count)], gpkr.at[pl.ds(0, count)], step).wait()
-
     def per_count(body):
         @pl.when(own)
         def _():
@@ -441,25 +438,10 @@
         def _():
             body(Z)
 
-    per_count(lambda count: gp_wait(count, gp_r, gpk_r))
+    per_count(lambda count: settle(gp_r, count * packed_bytes))
     gp_ref[...] = sum(unpack(gpr, gpkr, k) for k in range(Z))
 
-    def p_wait(count):
-        pltpu.make_async_copy(PB.at[0, pl.ds(0, count * n)], PB.at[0, pl.ds(0, count * n)], p_s).wait()
-        gp_wait(count, gp_s, gpk_s)
-
-    per_count(p_wait)
-    for ref, sem in (
-        (gqr, q_s),
-        (PB.at[0], f_s),
-        (W, w_s),
-        (crc, c_s),
-        (rrc, r_s),
-        (gqt, gq_s),
-        (gqk, gqk_s),
-        (Qs, h_s),
-    ):
-        pltpu.make_async_copy(ref, ref, sem).wait()
+    per_count(lambda count: settle(out_s, sent_bytes(n, w, Z, count == Z)))
 
 
 def local(queries, passages, positives):
@@ -495,6 +477,7 @@
             pltpu.VMEM((2 * Z - 1, 1, 2 * cols), F32),
             pltpu.VMEM((n, w), BF16),
             pltpu.VMEM((batch_count, n), jnp.int32),
+            pltpu.VMEM((1, sent_bytes(n, w, Z) // 4), F32),
             pltpu.VMEM((2, rows, w), F32),
             pltpu.VMEM((3, n, w), I16),
             pltpu.VMEM((3, n, w), I16),
@@ -510,26 +493,13 @@
             dma((3,)),
             dma,
             dma((2,)),
-            dma,
             dma((Z,)),
-            dma,
-            dma((Z,)),
-            dma,
-            dma,
-            dma,
-            dma,
+            dma((Z // 2,)),
             dma,
             dma,
             dma,
             dma((Z,)),
-            dma,
             dma((2,)),
-            dma,
-            dma,
-            dma,
-            dma((2,)),
-            dma,
-            dma,
             dma,
             dma,
         ],

time: 27.7 us -> 27.6 us (level)
  no operation moved by 1% of the time
where the time goes in v5:
time: 27.6 us; the launch traced here: 27.4 us
  Pallas kernels  26 us (94%)
  other arithmetic  0.72 us (3%)
  between operations  0.64 us (2%)
    pallas_call x1, Pallas kernels, local(): pl.pallas_call(functools.partial(kernel, Z, scale), out_shape=(jax.ShapeD...  26 us
    mul x1, other arithmetic, local(): return (grad_queries * scale, grad_passages * scale)  0.72 us

profile of v5, /device:TPU:0, one launch (start us, length us, event | category | flops | bytes accessed | tf_op | source)
XLA Modules:
  0.0 27.4 jit_solution(13418714897569739917)
XLA Ops:
  0.6 26.0 %shard_map.50 = (f32[128,256]{1,0:T(8,128)S(1)}, f32[128,256]{1,0:T(8,128)S(1)}) custom-call(bf16[128,256]{1,0:T(8,128)(2,1)} %q_ref.1, bf16[128,256]{1,0:T(8,128)(2,1)} %p_ref.1, s32[16,128]{1,0:T(8,128)} %bitcast.1), custom_call_target="tpu_custom_call" | custom-call | tf_op jit(solution)/shard_map/pallas_call | solution.py:458
  26.7 0.7 %broadcast_multiply_fusion = (f32[128,256]{1,0:T(8,128)}, f32[128,256]{1,0:T(8,128)}) fusion(f32[128,256]{1,0:T(8,128)S(1)} %get-tuple-element.5, f32[128,256]{1,0:T(8,128)S(1)} %get-tuple-element.4), kind=kLoop, calls=%fused_computation | loop fusion | flops 65536 | bytes 524288 | tf_op jit(solution)/shard_map/mul | solution.py:508

commit v6 on v5

--- a/solution.py
+++ b/solution.py
@@ -12,7 +12,7 @@
 F32 = jnp.float32
 BF16 = jnp.bfloat16
 I16 = jnp.int16
-TURNS = ((0, 1, 3, 2), (0, 3, 2, 1), (0, 3, 1, 2), (0, 2, 1, 3))
+TURNS = ((0, 1, 3, 2), (0, 3, 2, 1), (0, 3, 1, 2), (2, 0, 1, 3))
 
 
 def dot(a, b, da, db):
@@ -212,7 +212,7 @@
         pl.semaphore_wait(line.at[zz], 1)
         p_copy(zz).start()
 
-    @pl.when(jnp.logical_and(z > 0, z < Z - 1))
+    @pl.when(z < Z - 1)
     def _():
         send_later(z + 1)
 
@@ -221,10 +221,6 @@
         @pl.when(k > z + 1)
         def _():
             send_later(k)
-
-    @pl.when(z == 0)
-    def _():
-        send_later(1)
 
     answers = 2 * (Z - 1 - z) + c
 

time: 27.6 us -> 27.3 us (0.989)
  no operation moved by 1% of the time
where the time goes in v6:
time: 27.3 us; the launch traced here: 27.2 us
  Pallas kernels  25.8 us (95%)
  other arithmetic  0.72 us (3%)
  between operations  0.64 us (2%)
    pallas_call x1, Pallas kernels, local(): pl.pallas_call(functools.partial(kernel, Z, scale), out_shape=(jax.ShapeD...  25.8 us
    mul x1, other arithmetic, local(): return (grad_queries * scale, grad_passages * scale)  0.72 us

profile of v6, /device:TPU:0, one launch (start us, length us, event | category | flops | bytes accessed | tf_op | source)
XLA Modules:
  0.0 27.2 jit_solution(9722030877276176681)
XLA Ops:
  0.6 25.8 %shard_map.50 = (f32[128,256]{1,0:T(8,128)S(1)}, f32[128,256]{1,0:T(8,128)S(1)}) custom-call(bf16[128,256]{1,0:T(8,128)(2,1)} %q_ref.1, bf16[128,256]{1,0:T(8,128)(2,1)} %p_ref.1, s32[16,128]{1,0:T(8,128)} %bitcast.1), custom_call_target="tpu_custom_call" | custom-call | tf_op jit(solution)/shard_map/pallas_call | solution.py:454
  26.5 0.7 %broadcast_multiply_fusion = (f32[128,256]{1,0:T(8,128)}, f32[128,256]{1,0:T(8,128)}) fusion(f32[128,256]{1,0:T(8,128)S(1)} %get-tuple-element.5, f32[128,256]{1,0:T(8,128)S(1)} %get-tuple-element.4), kind=kLoop, calls=%fused_computation | loop fusion | flops 65536 | bytes 524288 | tf_op jit(solution)/shard_map/mul | solution.py:504

commit v7 on v6

--- a/solution.py
+++ b/solution.py
@@ -71,7 +71,6 @@
     q_r,
     p_r,
     f_r,
-    h_r,
     r_r,
     c_r,
     w_r,
@@ -120,9 +119,9 @@
     barrier = pltpu.get_barrier_semaphore()
 
     q_own = Q.at[x, span(y, n)]
-    p_in = pltpu.make_async_copy(p_ref, PM, in_s.at[0])
-    q_in = pltpu.make_async_copy(q_ref, q_own, in_s.at[1])
-    pos_in = pltpu.make_async_copy(pos_hbm, pos_ref, in_s.at[2])
+    p_in = pltpu.make_async_copy(p_ref, PM, in_s)
+    q_in = pltpu.make_async_copy(q_ref, q_own, in_s)
+    pos_in = pltpu.make_async_copy(pos_hbm, pos_ref, in_s)
     q_in.start()
     p_in.start()
     pos_in.start()
@@ -169,7 +168,7 @@
     def _():
         greet(line.at[z], target(z))
 
-    p_in.wait()
+    settle(in_s, 4 * n * w + 4 * pos_ref.shape[0] * n)
     p_block = PB.at[x, span(z, n)]
 
     def p_copy(zz):
@@ -184,9 +183,6 @@
         @pl.when(k < z)
         def _():
             p_copy(k).start()
-
-    q_in.wait()
-    pos_in.wait()
 
     @pl.when(own)
     def _():
@@ -212,7 +208,9 @@
         pl.semaphore_wait(line.at[zz], 1)
         p_copy(zz).start()
 
-    @pl.when(z < Z - 1)
+    nearest_last = jnp.logical_and(z > 0, jnp.logical_and(c == 0, x == 1))
+
+    @pl.when(jnp.logical_and(z < Z - 1, jnp.logical_not(nearest_last)))
     def _():
         send_later(z + 1)
 
@@ -221,6 +219,10 @@
         @pl.when(k > z + 1)
         def _():
             send_later(k)
+
+    @pl.when(jnp.logical_and(z < Z - 1, nearest_last))
+    def _():
+        send_later(z + 1)
 
     answers = 2 * (Z - 1 - z) + c
 
@@ -265,7 +267,7 @@
             total += running[1] * jnp.exp(running[0] - high)
         return high, total
 
-    half = remote(Q.at[c], Qs, out_s, h_r, sibling)
+    half = remote(Q.at[c], Qs, out_s, w_r.at[0], sibling)
 
     @pl.when(own)
     def _():
@@ -351,13 +353,13 @@
         high = lax.select(z == 2, jnp.int32(third_z), jnp.int32(fourth_z))
         return lax.select(z < 2, low, high)
 
-    def share(k):
-        return remote(W.at[k], Ws.at[k], out_s, w_r.at[k], sibling)
+    def share(i, k):
+        return remote(W.at[k], Ws.at[k], out_s, w_r.at[min(i, 1)], sibling)
 
     for i in range(Z):
         k = turn(i)
         W[k] = (A[k] + jnp.exp(S[:, span(k, n)] - crc[0, :, span(k, n)])).astype(BF16)
-        share(k).start()
+        share(i, k).start()
 
     def pack(value):
         top = jnp.maximum(jnp.max(jnp.abs(value), axis=0, keepdims=True), 1e-30)
@@ -395,12 +397,11 @@
 
     gq_send(1, gqp[x, span(1 - y, n), :], 1, gq_r.at[0], gq_r.at[0], beside)
 
-    half.wait_recv()
-
     for i in range(Z):
         k = turn(i)
         mine = dot(W[k], Q[1 - c], 0, 0)
-        share(k).wait_recv()
+        if i < 2:
+            settle(w_r.at[i], i * (Z - 1) * 2 * rows * n + (1 - i) * 2 * rows * (n + w))
         packed, step = pack(mine + dot(Ws[k], Qs[...], 0, 0))
         away = jnp.logical_or(z != k, crossed)
 
@@ -486,15 +487,14 @@
             regular((2,)),
             regular((Z,)),
             regular,
-            dma((3,)),
+            dma,
             dma,
             dma((2,)),
             dma((Z,)),
             dma((Z // 2,)),
             dma,
             dma,
-            dma,
-            dma((Z,)),
+            dma((2,)),
             dma((2,)),
             dma,
             dma,

time: 27.3 us -> 27.2 us (level)
  no operation moved by 1% of the time
where the time goes in v7:
time: 27.2 us; the launch traced here: 27 us
  Pallas kernels  25.6 us (94%)
  other arithmetic  0.72 us (3%)
  between operations  0.64 us (2%)
    pallas_call x1, Pallas kernels, local(): pl.pallas_call(functools.partial(kernel, Z, scale), out_shape=(jax.ShapeD...  25.6 us
    mul x1, other arithmetic, local(): return (grad_queries * scale, grad_passages * scale)  0.72 us

profile of v7, /device:TPU:0, one launch (start us, length us, event | category | flops | bytes accessed | tf_op | source)
XLA Modules:
  0.0 27.0 jit_solution(630883697392358248)
XLA Ops:
  0.6 25.6 %shard_map.50 = (f32[128,256]{1,0:T(8,128)S(1)}, f32[128,256]{1,0:T(8,128)S(1)}) custom-call(bf16[128,256]{1,0:T(8,128)(2,1)} %q_ref.1, bf16[128,256]{1,0:T(8,128)(2,1)} %p_ref.1, s32[16,128]{1,0:T(8,128)} %bitcast.1), custom_call_target="tpu_custom_call" | custom-call | tf_op jit(solution)/shard_map/pallas_call | solution.py:455
  26.3 0.7 %broadcast_multiply_fusion = (f32[128,256]{1,0:T(8,128)}, f32[128,256]{1,0:T(8,128)}) fusion(f32[128,256]{1,0:T(8,128)S(1)} %get-tuple-element.5, f32[128,256]{1,0:T(8,128)S(1)} %get-tuple-element.4), kind=kLoop, calls=%fused_computation | loop fusion | flops 65536 | bytes 524288 | tf_op jit(solution)/shard_map/mul | solution.py:504

commit v8 on v7

--- a/solution.py
+++ b/solution.py
@@ -389,13 +389,29 @@
     def gq_across(more):
         gq_send(2, gqp[1 - x, span(y, n), :] + more, 2, gq_r.at[1], gq_r.at[1], across)
 
+    def gq_beside():
+        gq_send(1, gqp[x, span(1 - y, n), :], 1, gq_r.at[0], gq_r.at[0], beside)
+
+    across_first = jnp.logical_and(c == 0, jnp.logical_and(y == 0, x == 1))
+    beside_first = jnp.logical_and(y == 1, x == 0)
+
+    @pl.when(across_first)
+    def _():
+        gq_across(0.0)
+
+    @pl.when(beside_first)
+    def _():
+        gq_beside()
+
     gq_send(0, gqp[1 - x, span(1 - y, n), :], 0, d_r, d_r, corner)
 
-    @pl.when(c == 0)
+    @pl.when(jnp.logical_and(c == 0, jnp.logical_not(across_first)))
     def _():
         gq_across(0.0)
 
-    gq_send(1, gqp[x, span(1 - y, n), :], 1, gq_r.at[0], gq_r.at[0], beside)
+    @pl.when(jnp.logical_not(beside_first))
+    def _():
+        gq_beside()
 
     for i in range(Z):
         k = turn(i)

time: 27.2 us -> 27 us (level)
  no operation moved by 1% of the time
where the time goes in v8:
time: 27 us; the launch traced here: 26.9 us
  Pallas kernels  25.5 us (94%)
  other arithmetic  0.72 us (3%)
  between operations  0.64 us (2%)
    pallas_call x1, Pallas kernels, local(): pl.pallas_call(functools.partial(kernel, Z, scale), out_shape=(jax.ShapeD...  25.5 us
    mul x1, other arithmetic, local(): return (grad_queries * scale, grad_passages * scale)  0.72 us

profile of v8, /device:TPU:0, one launch (start us, length us, event | category | flops | bytes accessed | tf_op | source)
XLA Modules:
  0.0 26.9 jit_solution(3478888397274018899)
XLA Ops:
  0.6 25.5 %shard_map.50 = (f32[128,256]{1,0:T(8,128)S(1)}, f32[128,256]{1,0:T(8,128)S(1)}) custom-call(bf16[128,256]{1,0:T(8,128)(2,1)} %q_ref.1, bf16[128,256]{1,0:T(8,128)(2,1)} %p_ref.1, s32[16,128]{1,0:T(8,128)} %bitcast.1), custom_call_target="tpu_custom_call" | custom-call | tf_op jit(solution)/shard_map/pallas_call | solution.py:471
  26.2 0.7 %broadcast_multiply_fusion = (f32[128,256]{1,0:T(8,128)}, f32[128,256]{1,0:T(8,128)}) fusion(f32[128,256]{1,0:T(8,128)S(1)} %get-tuple-element.5, f32[128,256]{1,0:T(8,128)S(1)} %get-tuple-element.4), kind=kLoop, calls=%fused_computation | loop fusion | flops 65536 | bytes 524288 | tf_op jit(solution)/shard_map/mul | solution.py:520

commit v9 on v8

--- a/solution.py
+++ b/solution.py
@@ -381,8 +381,7 @@
         remote(gqt.at[j], gqr.at[slot], out_s, data, device).start()
         remote(gqk.at[j], gqkr.at[slot], out_s, step, device).start()
 
-    for h in (0, 1):
-        gqp[h] = query_terms(h)
+    gqp[1 - x] = query_terms(1 - x)
     beside, across = dev(z, 1 - y, c, x), dev(z, y, c, 1 - x)
     corner = dev(z, 1 - y, c, lax.select(c == 1, x, 1 - x))
 
@@ -398,6 +397,8 @@
     @pl.when(across_first)
     def _():
         gq_across(0.0)
+
+    gqp[x] = query_terms(x)
 
     @pl.when(beside_first)
     def _():

time: 27 us -> 27 us (level)
  no operation moved by 1% of the time
where the time goes in v9:
time: 27 us; the launch traced here: 26.9 us
  Pallas kernels  25.5 us (94%)
  other arithmetic  0.72 us (3%)
  between operations  0.64 us (2%)
    pallas_call x1, Pallas kernels, local(): pl.pallas_call(functools.partial(kernel, Z, scale), out_shape=(jax.ShapeD...  25.5 us
    mul x1, other arithmetic, local(): return (grad_queries * scale, grad_passages * scale)  0.72 us

profile of v9, /device:TPU:0, one launch (start us, length us, event | category | flops | bytes accessed | tf_op | source)
XLA Modules:
  0.0 26.9 jit_solution(10648063761525559973)
XLA Ops:
  0.6 25.5 %shard_map.50 = (f32[128,256]{1,0:T(8,128)S(1)}, f32[128,256]{1,0:T(8,128)S(1)}) custom-call(bf16[128,256]{1,0:T(8,128)(2,1)} %q_ref.1, bf16[128,256]{1,0:T(8,128)(2,1)} %p_ref.1, s32[16,128]{1,0:T(8,128)} %bitcast.1), custom_call_target="tpu_custom_call" | custom-call | tf_op jit(solution)/shard_map/pallas_call | solution.py:472
  26.2 0.7 %broadcast_multiply_fusion = (f32[128,256]{1,0:T(8,128)}, f32[128,256]{1,0:T(8,128)}) fusion(f32[128,256]{1,0:T(8,128)S(1)} %get-tuple-element.5, f32[128,256]{1,0:T(8,128)S(1)} %get-tuple-element.4), kind=kLoop, calls=%fused_computation | loop fusion | flops 65536 | bytes 524288 | tf_op jit(solution)/shard_map/mul | solution.py:521
